TPU v7x, 32 devices: a whole 2x2x4 slice. The times are simulated.
32 devices in a mesh: cluster: 8 (over z, x), sub: 4 (over y, core).
Axes of the slice: x: 2, y: 2, z: 4, core: 2. Of those that a mesh axis runs over, the one named last changes fastest.
Arguments:
- mantissas: int32 [8, 64, 168, 128], P('cluster', 'sub'), may hold values from -128 to 127
- exponents: int32 [8, 64, 14], P('cluster', 'sub'), may hold values from -9 to -6
- channel: bfloat16 [8, 64, 2, 64, 128], P('cluster', 'sub'), may hold values from -0.5 to 0.5
- inverses: bfloat16 [8, 64, 2, 128, 128], P('cluster', 'sub'), may hold values from -4 to 4, as said below
Outputs:
- detected: bfloat16 [64, 168, 256], P('sub')
Inputs may be any that keep to these rules, and one draw needn't show every extreme that they name: `inverses`: each real part has a positive diagonal; the matrices are otherwise dense.
All inputs are finite; a program needn't handle non-finite values.
Results may differ from a plain program's by a relative error of at most 0.0074.
Values may be sent and summed in bfloat16 or wider, within the bound.
A program may use at most 64 MiB of HBM per device.

v0:
```python
import jax
import jax.numpy as jnp
from jax import lax
from jax.sharding import PartitionSpec as P

ITERS = 3
RHO = 0.5


def complex_block(real, imag):
    top = jnp.concatenate([real, -imag], axis=-1)
    bottom = jnp.concatenate([imag, real], axis=-1)
    return jnp.concatenate([top, bottom], axis=-2)


def per_device(mantissas, exponents, channel, inverses):
    clusters = lax.axis_size("cluster")
    mant = mantissas[0]
    blocks, vectors, _ = mant.shape
    expo = exponents[0]
    scale = jnp.repeat(jnp.exp2(expo.astype(jnp.float32)), vectors // expo.shape[1], axis=1)
    signal = (mant.astype(jnp.float32) * scale[:, :, None]).astype(jnp.bfloat16)
    match = complex_block(channel[0, :, 0], channel[0, :, 1])
    matched_filter = jnp.einsum("rsa,rau->rsu", signal, match, preferred_element_type=jnp.float32)
    solve_block = complex_block(inverses[0, :, 0], inverses[0, :, 1])
    width = matched_filter.shape[2]
    consensus = jnp.zeros(matched_filter.shape, jnp.float32)
    dual = jnp.zeros(matched_filter.shape, jnp.float32)
    for step in range(ITERS):
        rhs = (matched_filter + RHO * (consensus - dual)).astype(jnp.bfloat16)
        local = jnp.einsum("rsk,rjk->rsj", rhs, solve_block, preferred_element_type=jnp.float32)
        term = local + dual
        flat = term.reshape(blocks * vectors, width)
        share = lax.psum_scatter(flat, "cluster", scatter_dimension=0, tiled=True)
        average = (share / clusters).astype(jnp.bfloat16)
        gathered = lax.all_gather(average, "cluster", axis=0, tiled=True)
        consensus = gathered.reshape(blocks, vectors, width).astype(jnp.float32)
        dual = term - consensus
    users = width // 2
    column_list = jnp.sum(consensus * consensus, axis=(0, 1))
    partial_value = column_list[:users] + column_list[users:]
    total_power = lax.psum(partial_value, "sub")
    power = total_power / (blocks * lax.axis_size("sub") * vectors)
    factor = lax.rsqrt(power + 1e-06)
    factor = jnp.concatenate([factor, factor])
    return (consensus * factor).astype(jnp.bfloat16)


def solution(mesh):
    placed = (
        P("cluster", "sub", None, None),
        P("cluster", "sub", None),
        P("cluster", "sub", None, None, None),
        P("cluster", "sub", None, None, None),
    )
    return jax.shard_map(
        per_device, mesh=mesh, in_specs=placed, out_specs=P("sub", None, None), check_vma=False
    )
```

profile of v0, /device:TPU:0, one launch (start us, length us, event | category | flops | bytes accessed | tf_op | source)
XLA Modules:
  0.0 393.4 jit_solution(11023630587310864629)
XLA Ops:
  6.5 1.1 fusion.28
  7.6 1.1 slice_bitcast_fusion.2
  8.7 1.9 fusion.29
  10.6 1.1 slice_bitcast_fusion
  11.7 0.1 copy.15
  11.8 0.1 broadcast_in_dim.4
  11.9 0.1 mul.28
  12.0 2.0 fusion.15
  14.1 3.5 fusion.13
  17.6 0.0 reduce-scatter.4.cloned.1.call-update
  17.6 0.0 all-gather.4.cloned.1.call-start
  17.6 74.6 %reduce-scatter.4.cloned.1.call-done = f32[336,256]{1,0:T(8,128)} async-done(((f32[2688,256]{1,0:T(8,128)}), f32[336,256]{1,0:T(8,128)}) %reduce-scatter.4.cloned.1.call-update) | async-done | bytes 344080 | tf_op jit(solution)/shard_map/reduce_scatter | solution.py:34
  92.2 1.7 multiply_convert_fusion.3
  93.9 0.0 all-gather.4.cloned.1.call-update
  93.9 0.0 reduce-scatter.6.cloned.1.call-start
  94.0 41.8 %all-gather.4.cloned.1.call-done = bf16[2688,256]{1,0:T(8,128)(2,1)} async-done(((bf16[336,256]{1,0:T(8,128)(2,1)}), bf16[2688,256]{1,0:T(8,128)(2,1)}) %all-gather.4.cloned.1.call-update) | async-done | bytes 1376272 | tf_op jit(solution)/shard_map/all_gather | solution.py:36
  135.8 6.5 %fusion.6 = f32[16,168,256]{2,1,0:T(8,128)} fusion(f32[16,168,256]{2,1,0:T(8,128)} %fusion.13, bf16[16,168,256]{2,1,0:T(8,128)(2,1)} %bitcast.41, f32[16,168,256]{2,1,0:T(8,128)S(1)} %fusion.15, bf16[16,128,128]{2,1,0:T(8,128)(2,1)} %get-tuple-element.6, bf16[16,128,128]{2,1,0:T(8,128)(2,1)} %get-tuple-element.5, bf16[16,128,128]{2,1,0:T(8,128)(2,1)S(1)} %copy-done.1), kind=kOutput, calls=%fused_computation.12 | convolution fusion | flops 366903296 | bytes 11206656 | tf_op jit(solution)/shard_map/rsk,rjk->rsj/dot_general | solution.py:31
  142.2 0.0 reduce-scatter.6.cloned.1.call-update
  142.2 0.0 all-gather.6.cloned.1.call-start
  142.3 70.3 %reduce-scatter.6.cloned.1.call-done = f32[336,256]{1,0:T(8,128)} async-done(((f32[2688,256]{1,0:T(8,128)}), f32[336,256]{1,0:T(8,128)}) %reduce-scatter.6.cloned.1.call-update) | async-done | bytes 344080 | tf_op jit(solution)/shard_map/reduce_scatter | solution.py:34
  212.6 1.7 multiply_convert_fusion.2
  214.3 0.0 all-gather.6.cloned.1.call-update
  214.3 0.0 reduce-scatter.8.cloned.1.call-start
  214.4 41.6 %all-gather.6.cloned.1.call-done = bf16[2688,256]{1,0:T(8,128)(2,1)} async-done(((bf16[336,256]{1,0:T(8,128)(2,1)}), bf16[2688,256]{1,0:T(8,128)(2,1)}) %all-gather.6.cloned.1.call-update) | async-done | bytes 1376272 | tf_op jit(solution)/shard_map/all_gather | solution.py:36
  256.0 6.4 %fusion.7 = f32[16,168,256]{2,1,0:T(8,128)} fusion(f32[16,168,256]{2,1,0:T(8,128)} %fusion.6, bf16[16,168,256]{2,1,0:T(8,128)(2,1)} %bitcast.40, f32[16,168,256]{2,1,0:T(8,128)S(1)} %fusion.15, bf16[16,128,128]{2,1,0:T(8,128)(2,1)} %get-tuple-element.6, bf16[16,128,128]{2,1,0:T(8,128)(2,1)} %get-tuple-element.5, bf16[16,128,128]{2,1,0:T(8,128)(2,1)S(1)} %copy-done.1), kind=kOutput, calls=%fused_computation.13 | convolution fusion | flops 366903296 | bytes 11206656 | tf_op jit(solution)/shard_map/rsk,rjk->rsj/dot_general | solution.py:31
  262.4 0.0 all-gather.8.cloned.1.call-start
  262.4 70.7 %reduce-scatter.8.cloned.1.call-done = f32[336,256]{1,0:T(8,128)} async-done(((f32[2688,256]{1,0:T(8,128)}), f32[336,256]{1,0:T(8,128)}) %reduce-scatter.8.cloned.1.call-update) | async-done | bytes 344080 | tf_op jit(solution)/shard_map/reduce_scatter | solution.py:34
  333.2 1.7 multiply_convert_fusion.1
  334.9 41.6 %all-gather.8.cloned.1.call-done = bf16[2688,256]{1,0:T(8,128)(2,1)} async-done(((bf16[336,256]{1,0:T(8,128)(2,1)}), bf16[2688,256]{1,0:T(8,128)(2,1)}) %all-gather.8.cloned.1.call-update) | async-done | bytes 1376272 | tf_op jit(solution)/shard_map/all_gather | solution.py:36
  376.5 1.7 multiply_reduce_fusion
  378.2 5.7 %psum.7 = f32[128]{0:T(128)S(1)} all-reduce(f32[128]{0:T(128)S(1)} %slice_add_fusion), channel_id=1, replica_groups=mesh['cluster'=8,'sub'=4] {'sub'}, use_global_device_ids=true, to_apply=%region_4.0 | all-reduce | flops 128 | bytes 1024 | tf_op jit(solution)/shard_map/psum | solution.py:42
  383.9 2.7 multiply_convert_fusion
  (17 shorter events, 0.1 us)
Async XLA Ops:
  6.5 4.1 %copy-start = (bf16[1,16,2,128,128]{4,3,2,1,0:T(8,128)(2,1)S(1)}, bf16[1,16,2,128,128]{4,3,2,1,0:T(8,128)(2,1)}, u32[]{:S(2)}) copy-start(bf16[1,16,2,128,128]{4,3,2,1,0:T(8,128)(2,1)} %param.7) | copy-start | bytes 3145732
  6.5 5.2 %copy-start.4 = (s32[1,16,14]{1,0,2:T(1,128)S(1)}, s32[1,16,14]{1,0,2:T(1,128)}, u32[]{:S(2)}) copy-start(s32[1,16,14]{1,0,2:T(1,128)} %param.5) | copy-start | bytes 2692
  6.5 85.7 %reduce-scatter.4.cloned.1.call-start = ((), (), s32[]{:S(2)}) async-start(), calls=%async_computation.3 | async-start | bytes 3096576 | tf_op jit(solution)/shard_map/reduce_scatter | solution.py:34
  12.0 2.0 copy-start.2
  12.0 2.0 copy-start.3
  17.6 118.2 %copy-start.1 = (bf16[16,128,128]{2,1,0:T(8,128)(2,1)S(1)}, bf16[16,128,128]{2,1,0:T(8,128)(2,1)}, u32[]{:S(2)}) copy-start(bf16[16,128,128]{2,1,0:T(8,128)(2,1)} %fusion.29) | copy-start | bytes 1572868
  17.6 118.2 %all-gather.4.cloned.1.call-start = ((), (), s32[]{:S(2)}) async-start(), calls=%async_computation.4 | async-start | bytes 1548288 | tf_op jit(solution)/shard_map/all_gather | solution.py:36
  93.9 118.7 %reduce-scatter.6.cloned.1.call-start = ((), (), s32[]{:S(2)}) async-start(), calls=%async_computation.5 | async-start | bytes 3096576 | tf_op jit(solution)/shard_map/reduce_scatter | solution.py:34
  142.2 113.7 %all-gather.6.cloned.1.call-start = ((), (), s32[]{:S(2)}) async-start(), calls=%async_computation.6 | async-start | bytes 1548288 | tf_op jit(solution)/shard_map/all_gather | solution.py:36
  214.3 118.9 %reduce-scatter.8.cloned.1.call-start = ((), (), s32[]{:S(2)}) async-start(), calls=%async_computation.7 | async-start | bytes 3096576 | tf_op jit(solution)/shard_map/reduce_scatter | solution.py:34
  262.4 114.1 %all-gather.8.cloned.1.call-start = ((), (), s32[]{:S(2)}) async-start(), calls=%async_computation.8 | async-start | bytes 1548288 | tf_op jit(solution)/shard_map/all_gather | solution.py:36
Sparse Core Ops, SparseCore 0:
  17.7 74.4 reduce-scatter.3
  94.4 41.2 all-gather.3
  142.4 70.2 reduce-scatter.5
  214.7 41.2 all-gather.5
  262.5 70.6 reduce-scatter.7
  335.2 41.2 all-gather.7
where the time goes:
time: 394 us; the launch traced here: 393 us
  waiting for transfers between devices  341 us (87%)
  matrix products  18.4 us (5%)
  between operations  13.5 us (3%)
  other arithmetic  12.4 us (3%)
  blocking collectives  5.66 us (1%)
    reduce_scatter x3, waiting for transfers between devices, per_device(): share = lax.psum_scatter(flat, 'cluster', scatter_dimension=0, tiled=True)  216 us
    all_gather x3, waiting for transfers between devices, per_device(): gathered = lax.all_gather(average, 'cluster', axis=0, tiled=True)  125 us
    dot_general x3, matrix products, per_device(): jnp.einsum('rsk,rjk->rsj', rhs, solve_block, preferred_element_type=jnp.f...  16.4 us
  transfers between devices with their start and end apart: 6, of which 6 were waited for; matrix products, arithmetic and copies ran while one was open for 0% of the time, Pallas kernels for 0%

commit v1 on v0

--- a/solution.py
+++ b/solution.py
@@ -33,7 +33,13 @@
         flat = term.reshape(blocks * vectors, width)
         share = lax.psum_scatter(flat, "cluster", scatter_dimension=0, tiled=True)
         average = (share / clusters).astype(jnp.bfloat16)
-        gathered = lax.all_gather(average, "cluster", axis=0, tiled=True)
+        size = lax.axis_size("cluster")
+        held, parts = (average, [average])
+        for _ in range(size - 1):
+            held = lax.ppermute(held, "cluster", [(i, (i + 1) % size) for i in range(size)])
+            parts.insert(0, held)
+        line = jnp.concatenate(parts, axis=0)
+        gathered = jnp.roll(line, (lax.axis_index("cluster") + 1) * average.shape[0], axis=0)
         consensus = gathered.reshape(blocks, vectors, width).astype(jnp.float32)
         dual = term - consensus
     users = width // 2

time: 394 us -> 450 us (1.14)
  waiting for transfers between devices: 341 us -> 390 us
  matrix products: 18.4 us -> 8.77 us
  local copies, waits for them, and re-layouts: 2.45 us -> 9.52 us
  other arithmetic: 12.4 us -> 19.4 us
    ppermute x0 -> x21, waiting for transfers between devices: none -> 177 us  [per_device(): lax.ppermute(held, 'cluster', [(i, (i + 1) % size) for i in range(size)])]
    all_gather x3 -> x0, waiting for transfers between devices: 125 us -> none  [per_device(): gathered = lax.all_gather(average, 'cluster', axis=0, tiled=True)]
    dot_general x3, matrix products: 16.4 us -> 6.74 us  [per_device(): jnp.einsum('rsk,rjk->rsj', rhs, solve_block, preferred_element_type=jnp.f...]
    concatenate x0 -> x5, other arithmetic: none -> 8.42 us  [the longest x2 8.34 us: per_device(): jnp.roll(line, (lax.axis_index('cluster') + 1) * average.shape[0], axis=0)]
    unnamed x10 -> x59, local copies, waits for them, and re-layouts: 0.02 us -> 7.14 us
  transfers between devices with their start and end apart: 6 -> 24, of which waited for: 6 -> 24; matrix products, arithmetic and copies ran while one was open for 0% -> 0% of each run, Pallas kernels for 0% -> 0%
where the time goes in v1:
time: 450 us
  waiting for transfers between devices  390 us (87%)
  other arithmetic  19.4 us (4%)
  between operations  13.6 us (3%)
  local copies, waits for them, and re-layouts  9.52 us (2%)
  matrix products  8.77 us (2%)
  blocking collectives  5.67 us (1%)
    reduce_scatter x3, waiting for transfers between devices, per_device(): share = lax.psum_scatter(flat, 'cluster', scatter_dimension=0, tiled=True)  213 us
    ppermute x21, waiting for transfers between devices, per_device(): lax.ppermute(held, 'cluster', [(i, (i + 1) % size) for i in range(size)])  177 us
  transfers between devices with their start and end apart: 24, of which 24 were waited for; matrix products, arithmetic and copies ran while one was open for 0% of the time, Pallas kernels for 0%

profile of v1, /device:TPU:0, one launch (start us, length us, event | category | flops | bytes accessed | tf_op | source)
XLA Modules:
  0.0 449.7 jit_solution(15307624189901975374)
XLA Ops:
  12.0 2.0 fusion.19
  14.1 2.4 fusion.17
  16.5 74.6 %reduce-scatter.4.cloned.1.call-done = f32[336,256]{1,0:T(8,128)} async-done(((f32[2688,256]{1,0:T(8,128)}), f32[336,256]{1,0:T(8,128)}) %reduce-scatter.4.cloned.1.call-update) | async-done | bytes 344080 | tf_op jit(solution)/shard_map/reduce_scatter | solution.py:34
  93.2 7.1 %collective-permute-done = bf16[336,256]{1,0:T(8,128)(2,1)S(1)} collective-permute-done((bf16[336,256]{1,0:T(8,128)(2,1)S(1)}, bf16[336,256]{1,0:T(8,128)(2,1)S(1)}, u32[]{:S(2)}, u32[]{:S(2)}) %collective-permute-start) | collective-permute-done | bytes 172064 | tf_op jit(solution)/shard_map/ppermute | solution.py:39
  100.3 8.1 %collective-permute-done.1 = bf16[336,256]{1,0:T(8,128)(2,1)S(1)} collective-permute-done((bf16[336,256]{1,0:T(8,128)(2,1)S(1)}, bf16[336,256]{1,0:T(8,128)(2,1)S(1)}, u32[]{:S(2)}, u32[]{:S(2)}) %collective-permute-start.1) | collective-permute-done | bytes 172064 | tf_op jit(solution)/shard_map/ppermute | solution.py:39
  108.4 8.1 %collective-permute-done.2 = bf16[336,256]{1,0:T(8,128)(2,1)S(1)} collective-permute-done((bf16[336,256]{1,0:T(8,128)(2,1)S(1)}, bf16[336,256]{1,0:T(8,128)(2,1)S(1)}, u32[]{:S(2)}, u32[]{:S(2)}) %collective-permute-start.2) | collective-permute-done | bytes 172064 | tf_op jit(solution)/shard_map/ppermute | solution.py:39
  117.2 8.2 %collective-permute-done.3 = bf16[336,256]{1,0:T(8,128)(2,1)S(1)} collective-permute-done((bf16[336,256]{1,0:T(8,128)(2,1)S(1)}, bf16[336,256]{1,0:T(8,128)(2,1)S(1)}, u32[]{:S(2)}, u32[]{:S(2)}) %collective-permute-start.3) | collective-permute-done | bytes 172064 | tf_op jit(solution)/shard_map/ppermute | solution.py:39
  126.1 9.4 %collective-permute-done.4 = bf16[336,256]{1,0:T(8,128)(2,1)S(1)} collective-permute-done((bf16[336,256]{1,0:T(8,128)(2,1)S(1)}, bf16[336,256]{1,0:T(8,128)(2,1)S(1)}, u32[]{:S(2)}, u32[]{:S(2)}) %collective-permute-start.4) | collective-permute-done | bytes 172064 | tf_op jit(solution)/shard_map/ppermute | solution.py:39
  136.1 9.1 %collective-permute-done.5 = bf16[336,256]{1,0:T(8,128)(2,1)} collective-permute-done((bf16[336,256]{1,0:T(8,128)(2,1)S(1)}, bf16[336,256]{1,0:T(8,128)(2,1)}, u32[]{:S(2)}, u32[]{:S(2)}) %collective-permute-start.5) | collective-permute-done | bytes 172064 | tf_op jit(solution)/shard_map/ppermute | solution.py:39
  145.3 8.4 %collective-permute-done.6 = bf16[336,256]{1,0:T(8,128)(2,1)} collective-permute-done((bf16[336,256]{1,0:T(8,128)(2,1)}, bf16[336,256]{1,0:T(8,128)(2,1)}, u32[]{:S(2)}, u32[]{:S(2)}) %collective-permute-start.6) | collective-permute-done | bytes 172064 | tf_op jit(solution)/shard_map/ppermute | solution.py:39
  158.7 4.2 fusion.11
  162.9 2.2 fusion.6
  165.2 69.0 %reduce-scatter.6.cloned.1.call-done = f32[336,256]{1,0:T(8,128)} async-done(((f32[2688,256]{1,0:T(8,128)}), f32[336,256]{1,0:T(8,128)}) %reduce-scatter.6.cloned.1.call-update) | async-done | bytes 344080 | tf_op jit(solution)/shard_map/reduce_scatter | solution.py:34
  236.3 7.1 %collective-permute-done.7 = bf16[336,256]{1,0:T(8,128)(2,1)S(1)} collective-permute-done((bf16[336,256]{1,0:T(8,128)(2,1)S(1)}, bf16[336,256]{1,0:T(8,128)(2,1)S(1)}, u32[]{:S(2)}, u32[]{:S(2)}) %collective-permute-start.7) | collective-permute-done | bytes 172064 | tf_op jit(solution)/shard_map/ppermute | solution.py:39
  243.4 8.1 %collective-permute-done.8 = bf16[336,256]{1,0:T(8,128)(2,1)S(1)} collective-permute-done((bf16[336,256]{1,0:T(8,128)(2,1)S(1)}, bf16[336,256]{1,0:T(8,128)(2,1)S(1)}, u32[]{:S(2)}, u32[]{:S(2)}) %collective-permute-start.8) | collective-permute-done | bytes 172064 | tf_op jit(solution)/shard_map/ppermute | solution.py:39
  251.5 8.1 %collective-permute-done.9 = bf16[336,256]{1,0:T(8,128)(2,1)S(1)} collective-permute-done((bf16[336,256]{1,0:T(8,128)(2,1)S(1)}, bf16[336,256]{1,0:T(8,128)(2,1)S(1)}, u32[]{:S(2)}, u32[]{:S(2)}) %collective-permute-start.9) | collective-permute-done | bytes 172064 | tf_op jit(solution)/shard_map/ppermute | solution.py:39
  259.6 8.8 %collective-permute-done.10 = bf16[336,256]{1,0:T(8,128)(2,1)S(1)} collective-permute-done((bf16[336,256]{1,0:T(8,128)(2,1)S(1)}, bf16[336,256]{1,0:T(8,128)(2,1)S(1)}, u32[]{:S(2)}, u32[]{:S(2)}) %collective-permute-start.10) | collective-permute-done | bytes 172064 | tf_op jit(solution)/shard_map/ppermute | solution.py:39
  268.5 9.9 %collective-permute-done.11 = bf16[336,256]{1,0:T(8,128)(2,1)S(1)} collective-permute-done((bf16[336,256]{1,0:T(8,128)(2,1)S(1)}, bf16[336,256]{1,0:T(8,128)(2,1)S(1)}, u32[]{:S(2)}, u32[]{:S(2)}) %collective-permute-start.11) | collective-permute-done | bytes 172064 | tf_op jit(solution)/shard_map/ppermute | solution.py:39
  278.4 9.0 %collective-permute-done.12 = bf16[336,256]{1,0:T(8,128)(2,1)S(1)} collective-permute-done((bf16[336,256]{1,0:T(8,128)(2,1)S(1)}, bf16[336,256]{1,0:T(8,128)(2,1)S(1)}, u32[]{:S(2)}, u32[]{:S(2)}) %collective-permute-start.12) | collective-permute-done | bytes 172064 | tf_op jit(solution)/shard_map/ppermute | solution.py:39
  287.4 8.1 %collective-permute-done.13 = bf16[336,256]{1,0:T(8,128)(2,1)S(1)} collective-permute-done((bf16[336,256]{1,0:T(8,128)(2,1)S(1)}, bf16[336,256]{1,0:T(8,128)(2,1)S(1)}, u32[]{:S(2)}, u32[]{:S(2)}) %collective-permute-start.13) | collective-permute-done | bytes 172064 | tf_op jit(solution)/shard_map/ppermute | solution.py:39
  295.8 4.2 fusion.10
  300.0 2.2 fusion.7
  302.2 69.1 %reduce-scatter.8.cloned.1.call-done = f32[336,256]{1,0:T(8,128)} async-done(((f32[2688,256]{1,0:T(8,128)}), f32[336,256]{1,0:T(8,128)}) %reduce-scatter.8.cloned.1.call-update) | async-done | bytes 344080 | tf_op jit(solution)/shard_map/reduce_scatter | solution.py:34
  373.4 7.2 %collective-permute-done.14 = bf16[336,256]{1,0:T(8,128)(2,1)S(1)} collective-permute-done((bf16[336,256]{1,0:T(8,128)(2,1)S(1)}, bf16[336,256]{1,0:T(8,128)(2,1)S(1)}, u32[]{:S(2)}, u32[]{:S(2)}) %collective-permute-start.14) | collective-permute-done | bytes 172064 | tf_op jit(solution)/shard_map/ppermute | solution.py:39
  380.5 8.1 %collective-permute-done.15 = bf16[336,256]{1,0:T(8,128)(2,1)S(1)} collective-permute-done((bf16[336,256]{1,0:T(8,128)(2,1)S(1)}, bf16[336,256]{1,0:T(8,128)(2,1)S(1)}, u32[]{:S(2)}, u32[]{:S(2)}) %collective-permute-start.15) | collective-permute-done | bytes 172064 | tf_op jit(solution)/shard_map/ppermute | solution.py:39
  388.6 8.1 %collective-permute-done.16 = bf16[336,256]{1,0:T(8,128)(2,1)S(1)} collective-permute-done((bf16[336,256]{1,0:T(8,128)(2,1)S(1)}, bf16[336,256]{1,0:T(8,128)(2,1)S(1)}, u32[]{:S(2)}, u32[]{:S(2)}) %collective-permute-start.16) | collective-permute-done | bytes 172064 | tf_op jit(solution)/shard_map/ppermute | solution.py:39
  396.7 8.9 %collective-permute-done.17 = bf16[336,256]{1,0:T(8,128)(2,1)S(1)} collective-permute-done((bf16[336,256]{1,0:T(8,128)(2,1)S(1)}, bf16[336,256]{1,0:T(8,128)(2,1)S(1)}, u32[]{:S(2)}, u32[]{:S(2)}) %collective-permute-start.17) | collective-permute-done | bytes 172064 | tf_op jit(solution)/shard_map/ppermute | solution.py:39
  405.6 9.9 %collective-permute-done.18 = bf16[336,256]{1,0:T(8,128)(2,1)S(1)} collective-permute-done((bf16[336,256]{1,0:T(8,128)(2,1)S(1)}, bf16[336,256]{1,0:T(8,128)(2,1)S(1)}, u32[]{:S(2)}, u32[]{:S(2)}) %collective-permute-start.18) | collective-permute-done | bytes 172064 | tf_op jit(solution)/shard_map/ppermute | solution.py:39
  415.5 9.0 %collective-permute-done.19 = bf16[336,256]{1,0:T(8,128)(2,1)S(1)} collective-permute-done((bf16[336,256]{1,0:T(8,128)(2,1)S(1)}, bf16[336,256]{1,0:T(8,128)(2,1)S(1)}, u32[]{:S(2)}, u32[]{:S(2)}) %collective-permute-start.19) | collective-permute-done | bytes 172064 | tf_op jit(solution)/shard_map/ppermute | solution.py:39
  424.5 8.1 %collective-permute-done.20 = bf16[336,256]{1,0:T(8,128)(2,1)S(1)} collective-permute-done((bf16[336,256]{1,0:T(8,128)(2,1)S(1)}, bf16[336,256]{1,0:T(8,128)(2,1)S(1)}, u32[]{:S(2)}, u32[]{:S(2)}) %collective-permute-start.20) | collective-permute-done | bytes 172064 | tf_op jit(solution)/shard_map/ppermute | solution.py:39
  432.8 3.4 multiply_reduce_fusion
  436.2 5.7 %psum.7 = f32[128]{0:T(128)S(1)} all-reduce(f32[128]{0:T(128)S(1)} %slice_add_fusion), channel_id=1, replica_groups=mesh['cluster'=8,'sub'=4] {'sub'}, use_global_device_ids=true, to_apply=%region_4.6 | all-reduce | flops 128 | bytes 1024 | tf_op jit(solution)/shard_map/psum | solution.py:48
  (104 shorter events, 20.4 us)
Async XLA Ops:
  6.5 84.5 %reduce-scatter.4.cloned.1.call-start = ((), (), s32[]{:S(2)}) async-start(), calls=%async_computation.3 | async-start | bytes 3096576 | tf_op jit(solution)/shard_map/reduce_scatter | solution.py:34
  16.5 217.7 %reduce-scatter.6.cloned.1.call-start = ((), (), s32[]{:S(2)}) async-start(), calls=%async_computation.4 | async-start | bytes 3096576 | tf_op jit(solution)/shard_map/reduce_scatter | solution.py:34
  91.1 67.6 %copy-start.3 = (f32[336,256]{1,0:T(8,128)S(1)}, f32[336,256]{1,0:T(8,128)}, u32[]{:S(2)}) copy-start(f32[336,256]{1,0:T(8,128)} %reduce-scatter.4.cloned.1.call-done) | copy-start | bytes 1032196
  92.2 8.2 %collective-permute-start = (bf16[336,256]{1,0:T(8,128)(2,1)S(1)}, bf16[336,256]{1,0:T(8,128)(2,1)S(1)}, u32[]{:S(2)}, u32[]{:S(2)}) collective-permute-start(bf16[336,256]{1,0:T(8,128)(2,1)S(1)} %multiply_convert_fusion.3), channel_id=1, source_target_pairs={{0,4},{4,8},{8,12},{12,16},{16,20},{20,24},{24,28},{28,0},{1,5},{5... | collective-permute-start | bytes 516104 | tf_op jit(solution)/shard_map/ppermute | solution.py:39
  100.3 8.1 %collective-permute-start.1 = (bf16[336,256]{1,0:T(8,128)(2,1)S(1)}, bf16[336,256]{1,0:T(8,128)(2,1)S(1)}, u32[]{:S(2)}, u32[]{:S(2)}) collective-permute-start(bf16[336,256]{1,0:T(8,128)(2,1)S(1)} %collective-permute-done), channel_id=1, source_target_pairs={{0,4},{4,8},{8,12},{12,16},{16,20},{20,24},{24,28},{28,0},{1,5},{5... | collective-permute-start | bytes 516104 | tf_op jit(solution)/shard_map/ppermute | solution.py:39
  108.4 8.1 %collective-permute-start.2 = (bf16[336,256]{1,0:T(8,128)(2,1)S(1)}, bf16[336,256]{1,0:T(8,128)(2,1)S(1)}, u32[]{:S(2)}, u32[]{:S(2)}) collective-permute-start(bf16[336,256]{1,0:T(8,128)(2,1)S(1)} %collective-permute-done.1), channel_id=1, source_target_pairs={{0,4},{4,8},{8,12},{12,16},{16,20},{20,24},{24,28},{28,0},{1,5},{5... | collective-permute-start | bytes 516104 | tf_op jit(solution)/shard_map/ppermute | solution.py:39
  117.2 8.2 %collective-permute-start.3 = (bf16[336,256]{1,0:T(8,128)(2,1)S(1)}, bf16[336,256]{1,0:T(8,128)(2,1)S(1)}, u32[]{:S(2)}, u32[]{:S(2)}) collective-permute-start(bf16[336,256]{1,0:T(8,128)(2,1)S(1)} %collective-permute-done.2), channel_id=1, source_target_pairs={{0,4},{4,8},{8,12},{12,16},{16,20},{20,24},{24,28},{28,0},{1,5},{5... | collective-permute-start | bytes 516104 | tf_op jit(solution)/shard_map/ppermute | solution.py:39
  126.1 9.4 %collective-permute-start.4 = (bf16[336,256]{1,0:T(8,128)(2,1)S(1)}, bf16[336,256]{1,0:T(8,128)(2,1)S(1)}, u32[]{:S(2)}, u32[]{:S(2)}) collective-permute-start(bf16[336,256]{1,0:T(8,128)(2,1)S(1)} %collective-permute-done.3), channel_id=1, source_target_pairs={{0,4},{4,8},{8,12},{12,16},{16,20},{20,24},{24,28},{28,0},{1,5},{5... | collective-permute-start | bytes 516104 | tf_op jit(solution)/shard_map/ppermute | solution.py:39
  136.1 9.1 %collective-permute-start.5 = (bf16[336,256]{1,0:T(8,128)(2,1)S(1)}, bf16[336,256]{1,0:T(8,128)(2,1)}, u32[]{:S(2)}, u32[]{:S(2)}) collective-permute-start(bf16[336,256]{1,0:T(8,128)(2,1)S(1)} %collective-permute-done.4), channel_id=1, source_target_pairs={{0,4},{4,8},{8,12},{12,16},{16,20},{20,24},{24,28},{28,0},{1,5},{5... | collective-permute-start | bytes 516104 | tf_op jit(solution)/shard_map/ppermute | solution.py:39
  145.2 8.4 %collective-permute-start.6 = (bf16[336,256]{1,0:T(8,128)(2,1)}, bf16[336,256]{1,0:T(8,128)(2,1)}, u32[]{:S(2)}, u32[]{:S(2)}) collective-permute-start(bf16[336,256]{1,0:T(8,128)(2,1)} %collective-permute-done.5), channel_id=1, source_target_pairs={{0,4},{4,8},{8,12},{12,16},{16,20},{20,24},{24,28},{28,0},{1,5},{5... | collective-permute-start | bytes 516104 | tf_op jit(solution)/shard_map/ppermute | solution.py:39
  156.5 6.4 %copy-start.13 = (bf16[16,128,128]{2,1,0:T(8,128)(2,1)S(1)}, bf16[16,128,128]{2,1,0:T(8,128)(2,1)}, u32[]{:S(2)}) copy-start(bf16[16,128,128]{2,1,0:T(8,128)(2,1)} %get-tuple-element.9) | copy-start | bytes 1572868
  157.5 5.4 %copy-start = (f32[16,168,256]{2,1,0:T(8,128)S(1)}, f32[16,168,256]{2,1,0:T(8,128)}, u32[]{:S(2)}) copy-start(f32[16,168,256]{2,1,0:T(8,128)} %fusion.17) | copy-start | bytes 8257540
  157.5 5.4 %copy-start.7 = (bf16[16,128,128]{2,1,0:T(8,128)(2,1)S(1)}, bf16[16,128,128]{2,1,0:T(8,128)(2,1)}, u32[]{:S(2)}) copy-start(bf16[16,128,128]{2,1,0:T(8,128)(2,1)} %fusion.33) | copy-start | bytes 1572868
  157.5 5.4 %copy-start.10 = (bf16[16,128,128]{2,1,0:T(8,128)(2,1)S(1)}, bf16[16,128,128]{2,1,0:T(8,128)(2,1)}, u32[]{:S(2)}) copy-start(bf16[16,128,128]{2,1,0:T(8,128)(2,1)} %get-tuple-element.8) | copy-start | bytes 1572868
  165.1 206.2 %reduce-scatter.8.cloned.1.call-start = ((), (), s32[]{:S(2)}) async-start(), calls=%async_computation.5 | async-start | bytes 3096576 | tf_op jit(solution)/shard_map/reduce_scatter | solution.py:34
  234.2 61.5 %copy-start.4 = (f32[336,256]{1,0:T(8,128)S(1)}, f32[336,256]{1,0:T(8,128)}, u32[]{:S(2)}) copy-start(f32[336,256]{1,0:T(8,128)} %reduce-scatter.6.cloned.1.call-done) | copy-start | bytes 1032196
  235.3 8.2 %collective-permute-start.7 = (bf16[336,256]{1,0:T(8,128)(2,1)S(1)}, bf16[336,256]{1,0:T(8,128)(2,1)S(1)}, u32[]{:S(2)}, u32[]{:S(2)}) collective-permute-start(bf16[336,256]{1,0:T(8,128)(2,1)S(1)} %multiply_convert_fusion.2), channel_id=1, source_target_pairs={{0,4},{4,8},{8,12},{12,16},{16,20},{20,24},{24,28},{28,0},{1,5},{5... | collective-permute-start | bytes 516104 | tf_op jit(solution)/shard_map/ppermute | solution.py:39
  243.4 8.1 %collective-permute-start.8 = (bf16[336,256]{1,0:T(8,128)(2,1)S(1)}, bf16[336,256]{1,0:T(8,128)(2,1)S(1)}, u32[]{:S(2)}, u32[]{:S(2)}) collective-permute-start(bf16[336,256]{1,0:T(8,128)(2,1)S(1)} %collective-permute-done.7), channel_id=1, source_target_pairs={{0,4},{4,8},{8,12},{12,16},{16,20},{20,24},{24,28},{28,0},{1,5},{5... | collective-permute-start | bytes 516104 | tf_op jit(solution)/shard_map/ppermute | solution.py:39
  251.5 8.1 %collective-permute-start.9 = (bf16[336,256]{1,0:T(8,128)(2,1)S(1)}, bf16[336,256]{1,0:T(8,128)(2,1)S(1)}, u32[]{:S(2)}, u32[]{:S(2)}) collective-permute-start(bf16[336,256]{1,0:T(8,128)(2,1)S(1)} %collective-permute-done.8), channel_id=1, source_target_pairs={{0,4},{4,8},{8,12},{12,16},{16,20},{20,24},{24,28},{28,0},{1,5},{5... | collective-permute-start | bytes 516104 | tf_op jit(solution)/shard_map/ppermute | solution.py:39
  259.6 8.8 %collective-permute-start.10 = (bf16[336,256]{1,0:T(8,128)(2,1)S(1)}, bf16[336,256]{1,0:T(8,128)(2,1)S(1)}, u32[]{:S(2)}, u32[]{:S(2)}) collective-permute-start(bf16[336,256]{1,0:T(8,128)(2,1)S(1)} %collective-permute-done.9), channel_id=1, source_target_pairs={{0,4},{4,8},{8,12},{12,16},{16,20},{20,24},{24,28},{28,0},{1,5},{5... | collective-permute-start | bytes 516104 | tf_op jit(solution)/shard_map/ppermute | solution.py:39
  268.5 9.9 %collective-permute-start.11 = (bf16[336,256]{1,0:T(8,128)(2,1)S(1)}, bf16[336,256]{1,0:T(8,128)(2,1)S(1)}, u32[]{:S(2)}, u32[]{:S(2)}) collective-permute-start(bf16[336,256]{1,0:T(8,128)(2,1)S(1)} %collective-permute-done.10), channel_id=1, source_target_pairs={{0,4},{4,8},{8,12},{12,16},{16,20},{20,24},{24,28},{28,0},{1,5},{5... | collective-permute-start | bytes 516104 | tf_op jit(solution)/shard_map/ppermute | solution.py:39
  278.4 9.0 %collective-permute-start.12 = (bf16[336,256]{1,0:T(8,128)(2,1)S(1)}, bf16[336,256]{1,0:T(8,128)(2,1)S(1)}, u32[]{:S(2)}, u32[]{:S(2)}) collective-permute-start(bf16[336,256]{1,0:T(8,128)(2,1)S(1)} %collective-permute-done.11), channel_id=1, source_target_pairs={{0,4},{4,8},{8,12},{12,16},{16,20},{20,24},{24,28},{28,0},{1,5},{5... | collective-permute-start | bytes 516104 | tf_op jit(solution)/shard_map/ppermute | solution.py:39
  287.4 8.1 %collective-permute-start.13 = (bf16[336,256]{1,0:T(8,128)(2,1)S(1)}, bf16[336,256]{1,0:T(8,128)(2,1)S(1)}, u32[]{:S(2)}, u32[]{:S(2)}) collective-permute-start(bf16[336,256]{1,0:T(8,128)(2,1)S(1)} %collective-permute-done.12), channel_id=1, source_target_pairs={{0,4},{4,8},{8,12},{12,16},{16,20},{20,24},{24,28},{28,0},{1,5},{5... | collective-permute-start | bytes 516104 | tf_op jit(solution)/shard_map/ppermute | solution.py:39
  295.6 4.4 copy-start.14
  371.3 61.4 %copy-start.5 = (f32[336,256]{1,0:T(8,128)S(1)}, f32[336,256]{1,0:T(8,128)}, u32[]{:S(2)}) copy-start(f32[336,256]{1,0:T(8,128)} %reduce-scatter.8.cloned.1.call-done) | copy-start | bytes 1032196
  372.4 8.2 %collective-permute-start.14 = (bf16[336,256]{1,0:T(8,128)(2,1)S(1)}, bf16[336,256]{1,0:T(8,128)(2,1)S(1)}, u32[]{:S(2)}, u32[]{:S(2)}) collective-permute-start(bf16[336,256]{1,0:T(8,128)(2,1)S(1)} %multiply_convert_fusion.1), channel_id=1, source_target_pairs={{0,4},{4,8},{8,12},{12,16},{16,20},{20,24},{24,28},{28,0},{1,5},{5... | collective-permute-start | bytes 516104 | tf_op jit(solution)/shard_map/ppermute | solution.py:39
  380.5 8.1 %collective-permute-start.15 = (bf16[336,256]{1,0:T(8,128)(2,1)S(1)}, bf16[336,256]{1,0:T(8,128)(2,1)S(1)}, u32[]{:S(2)}, u32[]{:S(2)}) collective-permute-start(bf16[336,256]{1,0:T(8,128)(2,1)S(1)} %collective-permute-done.14), channel_id=1, source_target_pairs={{0,4},{4,8},{8,12},{12,16},{16,20},{20,24},{24,28},{28,0},{1,5},{5... | collective-permute-start | bytes 516104 | tf_op jit(solution)/shard_map/ppermute | solution.py:39
  388.6 8.1 %collective-permute-start.16 = (bf16[336,256]{1,0:T(8,128)(2,1)S(1)}, bf16[336,256]{1,0:T(8,128)(2,1)S(1)}, u32[]{:S(2)}, u32[]{:S(2)}) collective-permute-start(bf16[336,256]{1,0:T(8,128)(2,1)S(1)} %collective-permute-done.15), channel_id=1, source_target_pairs={{0,4},{4,8},{8,12},{12,16},{16,20},{20,24},{24,28},{28,0},{1,5},{5... | collective-permute-start | bytes 516104 | tf_op jit(solution)/shard_map/ppermute | solution.py:39
  396.7 8.9 %collective-permute-start.17 = (bf16[336,256]{1,0:T(8,128)(2,1)S(1)}, bf16[336,256]{1,0:T(8,128)(2,1)S(1)}, u32[]{:S(2)}, u32[]{:S(2)}) collective-permute-start(bf16[336,256]{1,0:T(8,128)(2,1)S(1)} %collective-permute-done.16), channel_id=1, source_target_pairs={{0,4},{4,8},{8,12},{12,16},{16,20},{20,24},{24,28},{28,0},{1,5},{5... | collective-permute-start | bytes 516104 | tf_op jit(solution)/shard_map/ppermute | solution.py:39
  405.6 9.9 %collective-permute-start.18 = (bf16[336,256]{1,0:T(8,128)(2,1)S(1)}, bf16[336,256]{1,0:T(8,128)(2,1)S(1)}, u32[]{:S(2)}, u32[]{:S(2)}) collective-permute-start(bf16[336,256]{1,0:T(8,128)(2,1)S(1)} %collective-permute-done.17), channel_id=1, source_target_pairs={{0,4},{4,8},{8,12},{12,16},{16,20},{20,24},{24,28},{28,0},{1,5},{5... | collective-permute-start | bytes 516104 | tf_op jit(solution)/shard_map/ppermute | solution.py:39
  415.5 9.0 %collective-permute-start.19 = (bf16[336,256]{1,0:T(8,128)(2,1)S(1)}, bf16[336,256]{1,0:T(8,128)(2,1)S(1)}, u32[]{:S(2)}, u32[]{:S(2)}) collective-permute-start(bf16[336,256]{1,0:T(8,128)(2,1)S(1)} %collective-permute-done.18), channel_id=1, source_target_pairs={{0,4},{4,8},{8,12},{12,16},{16,20},{20,24},{24,28},{28,0},{1,5},{5... | collective-permute-start | bytes 516104 | tf_op jit(solution)/shard_map/ppermute | solution.py:39
  424.5 8.1 %collective-permute-start.20 = (bf16[336,256]{1,0:T(8,128)(2,1)S(1)}, bf16[336,256]{1,0:T(8,128)(2,1)S(1)}, u32[]{:S(2)}, u32[]{:S(2)}) collective-permute-start(bf16[336,256]{1,0:T(8,128)(2,1)S(1)} %collective-permute-done.19), channel_id=1, source_target_pairs={{0,4},{4,8},{8,12},{12,16},{16,20},{20,24},{24,28},{28,0},{1,5},{5... | collective-permute-start | bytes 516104 | tf_op jit(solution)/shard_map/ppermute | solution.py:39
  (11 other events, 29.4 us)
Sparse Core Ops, SparseCore 0:
  16.6 74.4 reduce-scatter.3
  165.2 68.9 reduce-scatter.5
  302.3 68.9 reduce-scatter.7
